TPU v7x, 256 devices: a whole 4x4x8 slice. The times are simulated.
256 devices in a mesh: leaf: 32 (over z, x), rows: 8 (over y, core).
Axes of the slice: x: 4, y: 4, z: 8, core: 2. Of those that a mesh axis runs over, the one named last changes fastest.
Arguments:
- right_side: float32 [8, 262144], P(None, ('leaf', 'rows')), may hold values from -6 to 6
- diagonal: float32 [262144], P(('leaf', 'rows')), may hold values from 0.5 to 4
- tree_order: int32 [262144], P(('leaf', 'rows')), may hold values from 0 to 262143, as said below
- mid_perm: int32 [32], replicated, may hold values from 0 to 31, each once
- col_factor: bfloat16 [262144, 1536], P(('leaf', 'rows')), may hold values from -0.1875 to 0.1875
- mid_factor: bfloat16 [49152, 3072], P('leaf', 'rows'), may hold values from -0.0546875 to 0.0546875
- pre_factor: bfloat16 [49152, 3072], P('leaf', 'rows'), may hold values from -0.0546875 to 0.0546875
- row_factor: bfloat16 [48, 262144], P(None, ('leaf', 'rows')), may hold values from -0.875 to 0.875
Outputs:
- solution: float32 [8, 262144], P(None, ('leaf', 'rows'))
- residual: float32 [8, 262144], P(None, ('leaf', 'rows'))
Inputs may be any that keep to these rules, and one draw needn't show every extreme that they name: `tree_order`: each aligned run of 1024 entries, the run starting at b * 1024, is a permutation of b * 1024 to (b + 1) * 1024 - 1. `mid_perm`: a permutation of 0 to 31.
All inputs are finite; a program needn't handle non-finite values.
Results may differ from a plain program's by a relative error of at most 0.025.
Values may be sent and summed in bfloat16 or wider, within the bound.
A program may use at most 64 MiB of HBM per device.

v0:
```python
import jax
import jax.numpy as jnp
from jax import lax
from jax.experimental import pallas as pl
from jax.experimental.pallas import tpu as pltpu
from jax.sharding import PartitionSpec as P

F32, BF16 = jnp.float32, jnp.bfloat16
MESH = pl.DeviceIdType.MESH
SIDES, PTS, RANK, LEAVES, ROWB = 8, 1024, 48, 32, 8
Z, X = 8, 4
CHUNKS, EACH = 4, 8
GROUP = ROWB * RANK
LANES = 128
TILES = GROUP // LANES
APPLIES = 4


def ring_distance(step, size):
    return min(step, size - step)


LEAF_STEPS = sorted(
    ((dz, dx) for dz in range(Z) for dx in range(X) if dz or dx),
    key=lambda s: -(ring_distance(s[0], Z) + ring_distance(s[1], X)),
)
ROW_STEPS = sorted(range(1, ROWB), key=lambda s: -ring_distance(s, ROWB))


def three_parts(x):
    high = x.astype(BF16)
    rest = x - high.astype(F32)
    middle = rest.astype(BF16)
    low = (rest - middle.astype(F32)).astype(BF16)
    return high, middle, low


def nn_dot(a, b):
    return jnp.dot(a, b, preferred_element_type=F32)


def nt_dot(a, b):
    return lax.dot_general(a, b, (((1,), (1,)), ((), ())), preferred_element_type=F32)


def kernel(
    rs_hbm, diag_hbm, order_hbm, perm_hbm, col_hbm, mid_hbm, pre_hbm, row_hbm,
    x1_ref, p1_ref, r1_ref, image_ref, alpha_ref,
    rs, diag, order, perm, col, col_t, col_q, back_q, weight, returner, row_factor, onehot,
    field, scale, points, first_slots, slots, own_gram, gram_in, gram_high, gram_low, dots_out, dots_in, dots_sum,
    a_out, a_in, b_out, b_in, c_out, c_in,
    local_sem, gram_sems, dots_sems, a_send, a_recv, b_sems, c_send, c_recv,
):
    leaf, row = lax.axis_index("leaf"), lax.axis_index("rows")
    z, x = leaf // X, leaf % X
    own_chunk = z // 2
    leaf_peers = [lax.rem(z + dz, Z) * X + lax.rem(x + dx, X) for dz, dx in LEAF_STEPS]
    row_peers = [lax.rem(row + d, ROWB) for d in ROW_STEPS]
    barrier = pltpu.get_barrier_semaphore()
    for q in leaf_peers:
        pl.semaphore_signal(barrier, inc=1, device_id={"leaf": q}, device_id_type=MESH)
    for r in row_peers:
        pl.semaphore_signal(barrier, inc=1, device_id={"rows": r}, device_id_type=MESH)
    loads = []
    for i, (src, dst) in enumerate((
        (order_hbm, order), (rs_hbm, rs), (col_hbm, col), (row_hbm, row_factor), (perm_hbm, perm),
        (diag_hbm, diag), (pre_hbm, weight.at[0]), (mid_hbm, weight.at[1]),
    )):
        load = pltpu.make_async_copy(src, dst, local_sem.at[i])
        load.start()
        loads.append(load)
    l_order, l_rs, l_col, l_row, l_perm, l_diag = loads[:6]

    lane = lax.broadcasted_iota(jnp.int32, (SIDES, LANES), 1)
    zero = jnp.zeros((SIDES, LANES), F32)

    def chunk(step):
        return lax.rem(own_chunk + step, CHUNKS)

    turn = lax.rem(z, 2)
    far_z = (lax.rem(z + 4, Z), lax.rem(z + 5 - 2 * turn, Z))
    near_z = [lax.rem(z + 3 + 2 * turn, Z)] + [lax.rem(z + dz, Z) for dz in (2, 6, 1, 7, 0)]

    def by_distance(planes):
        hops = {2: 2, 1: 1, 3: 1, 0: 0}
        return [
            (zz, lax.rem(x + dx, X))
            for _, _, zz, dx in sorted(
                ((-(far + hops[dx]), i, zz, dx) for i, (far, zz) in enumerate(planes) for dx in hops if far or dx),
                key=lambda item: item[:2],
            )
        ]

    def group_of(zz):
        return lax.rem(zz // 2 - own_chunk + CHUNKS, 2)

    far_peers = by_distance(list(zip((4, 3), far_z)))
    near_peers = by_distance(list(zip((3, 2, 2, 1, 1, 0), near_z)))

    def slot_of(values, place, target):
        tile, offset = divmod(place * RANK, LANES)
        piece = values[:, tile * LANES : (tile + 1) * LANES]
        if offset + RANK > LANES:
            piece = jnp.where(lane >= offset, piece, values[:, (tile + 1) * LANES : (tile + 2) * LANES])
        shift = (target - offset) % LANES
        return pltpu.roll(piece, shift, 1) if shift else piece

    def leaf_send(apply, n, out, into, send, recv, q):
        pltpu.make_async_remote_copy(
            src_ref=out.at[apply, n], dst_ref=into.at[apply, leaf],
            send_sem=send.at[apply], recv_sem=recv, device_id={"leaf": q}, device_id_type=MESH,
        ).start()

    def put_slots(base, values, extra):
        for i in range(values.shape[1] // RANK):
            slots[base + i] = jnp.where(lane < RANK, slot_of(values, i, 0), extra)

    def send_peers(apply, start, peers, out, into, send, recv):
        for n, (zz, xx) in enumerate(peers):
            q = zz * X + xx
            out[apply, start + n] = slots[q].astype(BF16)
            leaf_send(apply, start + n, out, into, send, recv(zz), q)

    def leaf_wait(apply, count, into, send, recv):
        part = into.at[apply, pl.ds(0, count)]
        pltpu.make_async_remote_copy(
            src_ref=part, dst_ref=part, send_sem=send.at[apply], recv_sem=recv,
            device_id={"leaf": leaf_peers[0]}, device_id_type=MESH,
        ).wait_recv()

    def joined(apply, base, into):
        tiles = [None] * TILES

        def put(tile, value):
            tiles[tile] = value if tiles[tile] is None else tiles[tile] + value

        for i in range(EACH):
            tile, offset = divmod(i * RANK, LANES)
            value = jnp.where(lane < RANK, into[apply, base + i].astype(F32), 0.0)
            if offset:
                value = pltpu.roll(value, offset, 1)
            if offset + RANK > LANES:
                put(tile, jnp.where(lane >= offset, value, 0.0))
                put(tile + 1, jnp.where(lane < offset, value, 0.0))
            else:
                put(tile, value)
        return jnp.concatenate(tiles, axis=1).astype(BF16)

    def rows_copy(src, dst, sems, r):
        return pltpu.make_async_remote_copy(
            src_ref=src, dst_ref=dst, send_sem=sems.at[0], recv_sem=sems.at[1],
            device_id={"rows": r}, device_id_type=MESH,
        )

    def rows_wait(into, sems):
        part = into.at[pl.ds(0, ROWB - 1)]
        return rows_copy(part, part, sems, row_peers[0])

    def summed(into):
        total = into[0]
        for r in range(1, ROWB):
            total = total + into[r]
        return total

    def side_sum(products):
        return jnp.sum(products, axis=1, keepdims=True)

    def to_points(values):
        parts = [nt_dot(part, onehot[...]) for part in three_parts(values)]
        return (parts[0] + parts[1]) + parts[2]

    l_order.wait()
    local_index = order[...] % PTS
    step = 128
    for start in range(0, PTS, step):
        point = lax.broadcasted_iota(jnp.int32, (step, PTS), 0) + start
        onehot[pl.ds(start, step), :] = jnp.where(point == local_index, 1.0, 0.0).astype(BF16)
    l_rs.wait()
    rs_high, rs_middle, rs_low = three_parts(rs[...])
    tree_high = nn_dot(rs_high, onehot[...])
    l_col.wait()
    values = nn_dot(tree_high.astype(BF16), col[...])
    for g in range(LEAVES):
        tile, offset = divmod(g * RANK, LANES)
        piece = values[:, tile * LANES : (tile + 1) * LANES]
        if offset + RANK > LANES:
            piece = jnp.where(lane >= offset, piece, values[:, (tile + 1) * LANES : (tile + 2) * LANES])
        if offset:
            piece = pltpu.roll(piece, LANES - offset, 1)
        first_slots[g] = jnp.where(lane < RANK, piece, 0.0)
    l_perm.wait()
    l_row.wait()
    pl.semaphore_wait(barrier, len(LEAF_STEPS) + len(ROW_STEPS))
    for n, q in enumerate(leaf_peers):
        a_out[0, n] = first_slots[perm[q]].astype(BF16)
        leaf_send(0, n, a_out, a_in, a_send, a_recv.at[0], q)
    a_in[0, leaf] = first_slots[perm[leaf]].astype(BF16)

    @pl.when(leaf >= 0)
    def _():
        gram = nt_dot(row_factor[...], row_factor[...])
        own_gram[...] = jnp.concatenate([gram, jnp.zeros((RANK, LANES - RANK), F32)], axis=1)
        for r in row_peers:
            rows_copy(own_gram, gram_in.at[row], gram_sems, r).start()
        gram_in[row] = own_gram[...]

    @pl.when(leaf >= 0)
    def _():
        tree_middle = nn_dot(jnp.concatenate([rs_middle, rs_low], axis=0), onehot[...])
        field[0] = (tree_high + tree_middle[:SIDES]) + tree_middle[SIDES:]
        for t in range(LEAVES * RANK // LANES):
            turned = col[:, t * LANES : (t + 1) * LANES].T
            start = 0
            while start < LANES:
                g, first = divmod(t * LANES + start, RANK)
                count = min(RANK - first, LANES - start)
                col_t[g, pl.ds(first, count), :] = turned[start : start + count]
                start += count
        for q in range(LEAVES):
            c, i = divmod(q, EACH)
            back_q[0, c, pl.ds(i * RANK, RANK), :] = col_t[perm[q]]
        l_diag.wait()
        diag_points = jnp.broadcast_to(diag[...], (SIDES, PTS))
        diag_tree = [nn_dot(part, onehot[...]) for part in three_parts(diag_points)]
        diag_tree = (diag_tree[0] + diag_tree[1]) + diag_tree[2]
        scale[0] = 1.0 / diag_tree
        scale[1] = diag_tree
        for load in loads[6:]:
            load.wait()


    def build_gram():
        rows_wait(gram_in, gram_sems).wait_recv()
        wide = lax.broadcasted_iota(jnp.int32, (RANK, LANES), 1)
        for j in range(ROWB):
            tile, offset = divmod(j * RANK, LANES)
            value = gram_in[j]
            if offset:
                value = pltpu.roll(value, offset, 1)
            parts = [jnp.zeros((RANK, LANES), F32)] * TILES
            if offset + RANK > LANES:
                parts[tile] = jnp.where(wide >= offset, value, 0.0)
                parts[tile + 1] = jnp.where(wide < offset, value, 0.0)
            else:
                parts[tile] = value
            whole = jnp.concatenate(parts, axis=1)
            high = whole.astype(BF16)
            gram_high[pl.ds(j * RANK, RANK), :] = high
            gram_low[pl.ds(j * RANK, RANK), :] = (whole - high.astype(F32)).astype(BF16)

    def build_returner(kind):
        for c in range(CHUNKS):
            rows = pl.ds(c * GROUP, GROUP)
            product = nt_dot(gram_high[...], weight[kind, rows]) + nt_dot(gram_low[...], weight[kind, rows])
            returner[kind, :, c * GROUP : (c + 1) * GROUP] = product.astype(BF16)

    def build_last(chunks):
        for c in chunks:
            back_q[1, c] = nt_dot(back_q[0, c], onehot[...]).astype(BF16)

    earlier_head = None
    dots_total = None
    for apply in range(APPLIES):
        kind, last = apply % 2, apply == APPLIES - 1
        @pl.when(leaf >= 0)
        def _():
            if 0 < apply:
                points[apply] = to_points(field[apply])
            if last:
                r0, z0, w0, y, d = field[0], field[1], field[2], field[3], scale[1]
                out = zero
                for i, products in enumerate([r0 * z0, z0 * w0, r0 * y, w0 * y, d * z0 * y, d * y * y]):
                    out = jnp.where(lane == i, side_sum(products), out)
                dots_out[...] = out
                for r in row_peers:
                    rows_copy(dots_out, dots_in.at[row], dots_sems, r).start()
                dots_in[row] = out

        leaf_wait(apply, LEAVES - 1, a_in, a_send, a_recv.at[apply])
        incoming = jnp.concatenate([joined(apply, c * EACH, a_in) for c in range(CHUNKS)], axis=1)
        partial = nn_dot(incoming, weight[kind])
        b_out[apply] = partial
        for r in row_peers:
            rows_copy(b_out.at[apply], b_in.at[apply, row], b_sems.at[apply], r).start()
        b_in[apply, row] = partial
        @pl.when(leaf >= 0)
        def _():
            if apply == 0:
                build_gram()
                build_returner(0)
            if last:
                rows_wait(dots_in, dots_sems).wait_recv()
                dots_sum[...] = summed(dots_in)

        rows_wait(b_in.at[apply], b_sems.at[apply]).wait_recv()
        head = summed(b_in.at[apply]).astype(BF16)
        extra = zero
        if apply == 1:
            earlier_head = head.astype(F32)
        if last:
            back = nn_dot(head, gram_high[...]) + nn_dot(head, gram_low[...])
            dots = jnp.where(lane == 6, side_sum(earlier_head * back), dots_sum[...])
            dots = jnp.where(lane == 7, side_sum(head.astype(F32) * back), dots)
            high, middle, low = three_parts(dots)
            extra = (
                pltpu.roll(high.astype(F32), 64, 1)
                + pltpu.roll(middle.astype(F32), 72, 1)
                + pltpu.roll(low.astype(F32), 80, 1)
            )
        put_slots(0, nn_dot(head, returner[kind]), extra)
        send_peers(apply, 0, far_peers, c_out, c_in, c_send, lambda zz: c_recv.at[apply, 2])
        send_peers(apply, EACH, near_peers, c_out, c_in, c_send, lambda zz: c_recv.at[apply, group_of(zz)])
        c_in[apply, leaf] = slots[leaf].astype(BF16)
        @pl.when(leaf >= 0)
        def _():
            if apply == 0:
                for c in range(CHUNKS):
                    col_q[c] = back_q[0, c].T
                build_returner(1)
            if apply in (1, 2):
                build_last((0, 1) if apply == 1 else (2, 3))

        image = None
        for group, (steps, count) in enumerate((((0,), EACH - 1), ((1, 3), 2 * EACH), ((2,), EACH))):
            leaf_wait(apply, count, c_in, c_send, c_recv.at[apply, group])
            for step in steps:
                c = chunk(step)
                product = nn_dot(joined(apply, c * EACH, c_in), back_q[1 if last else 0, c])
                image = product if image is None else image + product
                if last:
                    for i in range(EACH):
                        value = c_in[apply, c * EACH + i].astype(F32)
                        dots_total = value if dots_total is None else dots_total + value
        if not last:
            following = scale[kind] * field[apply] + image
            field[apply + 1] = following
            taken = following.astype(BF16)
            c = chunk(2)
            put_slots(c * EACH, nn_dot(taken, col_q[c]), zero)
            send_peers(apply + 1, 0, far_peers, a_out, a_in, a_send, lambda zz: a_recv.at[apply + 1])
            others = [(chunk(step), nn_dot(taken, col_q[chunk(step)])) for step in (1, 3, 0)]
            for c, values in others:
                put_slots(c * EACH, values, zero)
            send_peers(apply + 1, EACH, near_peers, a_out, a_in, a_send, lambda zz: a_recv.at[apply + 1])
            a_in[apply + 1, leaf] = slots[leaf].astype(BF16)

    def dot_value(i):
        return (
            dots_total[:, 64 + i : 65 + i] + dots_total[:, 72 + i : 73 + i] + dots_total[:, 80 + i : 81 + i]
        )

    rz, zw, ry, wy = (dot_value(i) for i in range(4))
    zt, yt = dot_value(4) + dot_value(6), dot_value(5) + dot_value(7)
    alpha = rz / zw
    rz_next = (rz - alpha * zw) - alpha * (ry - alpha * wy)
    along = 1.0 + rz_next / rz
    alpha_next = rz_next / (along * along * zw - along * alpha * (zt + wy) + alpha * alpha * yt)
    z0, w0, y = points[1], points[2], points[3]
    t = diag[...] * y + image
    x1_ref[...] = alpha * z0
    p1_ref[...] = along * z0 - alpha * y
    r1_ref[...] = rs[...] - alpha * w0
    image_ref[...] = along * w0 - alpha * t
    alpha_ref[...] = jnp.broadcast_to(alpha_next, (SIDES, PTS))

    for r in row_peers:
        rows_copy(own_gram, gram_in.at[row], gram_sems, r).wait_send()
        rows_copy(dots_out, dots_in.at[row], dots_sems, r).wait_send()
    for apply in range(APPLIES):
        for out, send in ((a_out, a_send), (c_out, c_send)):
            pltpu.make_async_remote_copy(
                src_ref=out.at[apply], dst_ref=out.at[apply],
                send_sem=send.at[apply], recv_sem=a_recv.at[apply],
                device_id={"leaf": leaf_peers[0]}, device_id_type=MESH,
            ).wait_send()
        for r in row_peers:
            rows_copy(b_out.at[apply], b_in.at[apply, row], b_sems.at[apply], r).wait_send()


def per_device(
    right_side, diagonal, tree_order, mid_perm, col_factor, mid_factor, pre_factor, row_factor
):
    hbm = pl.BlockSpec(memory_space=pl.ANY)
    vmem = pl.BlockSpec(memory_space=pltpu.VMEM)
    diagonal, tree_order = diagonal.reshape(1, PTS), tree_order.reshape(1, PTS)
    right_side, diagonal, tree_order, mid_perm, col_factor, mid_factor, pre_factor, row_factor = (
        pltpu.with_memory_space_constraint(array, pltpu.HBM)
        for array in (right_side, diagonal, tree_order, mid_perm, col_factor, mid_factor, pre_factor, row_factor)
    )
    x1, p1, r1, image, alpha = pl.pallas_call(
        kernel,
        out_shape=(jax.ShapeDtypeStruct((SIDES, PTS), F32),) * 5,
        in_specs=[hbm] * 8,
        out_specs=(vmem,) * 5,
        scratch_shapes=[
            pltpu.VMEM((SIDES, PTS), F32),
            pltpu.VMEM((1, PTS), F32),
            pltpu.VMEM((1, PTS), jnp.int32),
            pltpu.SMEM((LEAVES,), jnp.int32),
            pltpu.VMEM((PTS, LEAVES * RANK), BF16),
            pltpu.VMEM((LEAVES, RANK, PTS), BF16),
            pltpu.VMEM((CHUNKS, PTS, GROUP), BF16),
            pltpu.VMEM((2, CHUNKS, GROUP, PTS), BF16),
            pltpu.VMEM((2, LEAVES * RANK, GROUP), BF16),
            pltpu.VMEM((2, GROUP, LEAVES * RANK), BF16),
            pltpu.VMEM((RANK, PTS), BF16),
            pltpu.VMEM((PTS, PTS), BF16),
            pltpu.VMEM((APPLIES, SIDES, PTS), F32),
            pltpu.VMEM((2, SIDES, PTS), F32),
            pltpu.VMEM((APPLIES, SIDES, PTS), F32),
            pltpu.VMEM((LEAVES, SIDES, LANES), F32),
            pltpu.VMEM((LEAVES, SIDES, LANES), F32),
            pltpu.VMEM((RANK, LANES), F32),
            pltpu.VMEM((ROWB, RANK, LANES), F32),
            pltpu.VMEM((GROUP, GROUP), BF16),
            pltpu.VMEM((GROUP, GROUP), BF16),
            pltpu.VMEM((SIDES, LANES), F32),
            pltpu.VMEM((ROWB, SIDES, LANES), F32),
            pltpu.VMEM((SIDES, LANES), F32),
            pltpu.VMEM((APPLIES, LEAVES - 1, SIDES, LANES), BF16),
            pltpu.VMEM((APPLIES, LEAVES, SIDES, LANES), BF16),
            pltpu.VMEM((APPLIES, SIDES, GROUP), F32),
            pltpu.VMEM((APPLIES, ROWB, SIDES, GROUP), F32),
            pltpu.VMEM((APPLIES, LEAVES - 1, SIDES, LANES), BF16),
            pltpu.VMEM((APPLIES, LEAVES, SIDES, LANES), BF16),
            pltpu.SemaphoreType.DMA((8,)),
            pltpu.SemaphoreType.DMA((2,)),
            pltpu.SemaphoreType.DMA((2,)),
            pltpu.SemaphoreType.DMA((APPLIES,)),
            pltpu.SemaphoreType.DMA((APPLIES,)),
            pltpu.SemaphoreType.DMA((APPLIES, 2)),
            pltpu.SemaphoreType.DMA((APPLIES,)),
            pltpu.SemaphoreType.DMA((APPLIES, 3)),
        ],
        compiler_params=pltpu.CompilerParams(
            collective_id=0, has_side_effects=True, vmem_limit_bytes=40000 * 1024
        ),
    )(
        right_side, diagonal, tree_order, mid_perm,
        col_factor, mid_factor, pre_factor, row_factor,
    )
    return x1 + alpha * p1, r1 - alpha * image


def solution(mesh):
    every = ("leaf", "rows")
    return jax.shard_map(
        per_device,
        mesh=mesh,
        in_specs=(
            P(None, every), P(every), P(every), P(),
            P(every, None), P("leaf", "rows"), P("leaf", "rows"), P(None, every),
        ),
        out_specs=(P(None, every), P(None, every)),
        check_vma=False,
    )
```

profile of v0, /device:TPU:1, one launch (start us, length us, event | category | flops | bytes accessed | tf_op | source)
XLA Modules:
  0.0 78.7 jit_solution(12478869270497593801)
XLA Ops:
  0.6 77.4 %shard_map.95 = (f32[8,1024]{1,0:T(8,128)S(1)}, f32[8,1024]{1,0:T(8,128)S(1)}, f32[8,1024]{1,0:T(8,128)S(1)}, f32[8,1024]{1,0:T(8,128)S(1)}, f32[8,1024]{1,0:T(8,128)S(1)}) custom-call(f32[8,1024]{1,0:T(8,128)} %rs_hbm.1, f32[1,1024]{1,0:T(1,128)} %bitcast.2, s32[1,1024]{1,0:T(1,128)} %bitcast.3, s32[32]{0:T(128)} %perm_hbm.1, bf16[1024,1536]{1,0:T(8,128)(2,1)} %col_hbm.1, ...), custom_call_target="tpu_custom_call" | custom-call | tf_op jit(solution)/shard_map/pallas_call | solution.py:390
  78.0 0.6 multiply_subtract_fusion
where the time goes:
time: 78.8 us; the launch traced here: 78.7 us
  Pallas kernels  77.4 us (98%)
    pallas_call x1, Pallas kernels, per_device(): pl.pallas_call(kernel, out_shape=(jax.ShapeDtypeStruct((SIDES, PTS), F32)...  77.4 us

commit v1 on v0

--- a/solution.py
+++ b/solution.py
@@ -9,10 +9,12 @@
 MESH = pl.DeviceIdType.MESH
 SIDES, PTS, RANK, LEAVES, ROWB = 8, 1024, 48, 32, 8
 Z, X = 8, 4
-CHUNKS, EACH = 4, 8
+PLANE = X * RANK
+FAR_TURNS, NEAR_TURNS = (4, 3, 5), (0, 1, 7, 2, 6)
 GROUP = ROWB * RANK
 LANES = 128
 TILES = GROUP // LANES
+FAR_COUNT, NEAR_COUNT = 3 * X, 5 * X - 1
 APPLIES = 4
 
 
@@ -53,7 +55,6 @@
 ):
     leaf, row = lax.axis_index("leaf"), lax.axis_index("rows")
     z, x = leaf // X, leaf % X
-    own_chunk = z // 2
     leaf_peers = [lax.rem(z + dz, Z) * X + lax.rem(x + dx, X) for dz, dx in LEAF_STEPS]
     row_peers = [lax.rem(row + d, ROWB) for d in ROW_STEPS]
     barrier = pltpu.get_barrier_semaphore()
@@ -74,36 +75,15 @@
     lane = lax.broadcasted_iota(jnp.int32, (SIDES, LANES), 1)
     zero = jnp.zeros((SIDES, LANES), F32)
 
-    def chunk(step):
-        return lax.rem(own_chunk + step, CHUNKS)
-
-    turn = lax.rem(z, 2)
-    far_z = (lax.rem(z + 4, Z), lax.rem(z + 5 - 2 * turn, Z))
-    near_z = [lax.rem(z + 3 + 2 * turn, Z)] + [lax.rem(z + dz, Z) for dz in (2, 6, 1, 7, 0)]
-
-    def by_distance(planes):
-        hops = {2: 2, 1: 1, 3: 1, 0: 0}
-        return [
-            (zz, lax.rem(x + dx, X))
-            for _, _, zz, dx in sorted(
-                ((-(far + hops[dx]), i, zz, dx) for i, (far, zz) in enumerate(planes) for dx in hops if far or dx),
-                key=lambda item: item[:2],
-            )
-        ]
-
-    def group_of(zz):
-        return lax.rem(zz // 2 - own_chunk + CHUNKS, 2)
-
-    far_peers = by_distance(list(zip((4, 3), far_z)))
-    near_peers = by_distance(list(zip((3, 2, 2, 1, 1, 0), near_z)))
-
-    def slot_of(values, place, target):
+    def plane(turn):
+        return lax.rem(z + turn, Z)
+
+    def slot_of(values, place):
         tile, offset = divmod(place * RANK, LANES)
         piece = values[:, tile * LANES : (tile + 1) * LANES]
         if offset + RANK > LANES:
             piece = jnp.where(lane >= offset, piece, values[:, (tile + 1) * LANES : (tile + 2) * LANES])
-        shift = (target - offset) % LANES
-        return pltpu.roll(piece, shift, 1) if shift else piece
+        return pltpu.roll(piece, LANES - offset, 1) if offset else piece
 
     def leaf_send(apply, n, out, into, send, recv, q):
         pltpu.make_async_remote_copy(
@@ -112,14 +92,15 @@
         ).start()
 
     def put_slots(base, values, extra):
-        for i in range(values.shape[1] // RANK):
-            slots[base + i] = jnp.where(lane < RANK, slot_of(values, i, 0), extra)
-
-    def send_peers(apply, start, peers, out, into, send, recv):
-        for n, (zz, xx) in enumerate(peers):
-            q = zz * X + xx
-            out[apply, start + n] = slots[q].astype(BF16)
-            leaf_send(apply, start + n, out, into, send, recv(zz), q)
+        for i in range(X if values.shape[1] == 2 * LANES else LEAVES):
+            slots[base + i] = jnp.where(lane < RANK, slot_of(values, i), extra)
+
+    def send_peers(apply, turns, out, into, send, recv):
+        for n, (dz, dx) in enumerate(LEAF_STEPS):
+            if dz in turns:
+                q = leaf_peers[n]
+                out[apply, n] = slots[q].astype(BF16)
+                leaf_send(apply, n, out, into, send, recv.at[apply, int(dz in FAR_TURNS)], q)
 
     def leaf_wait(apply, count, into, send, recv):
         part = into.at[apply, pl.ds(0, count)]
@@ -128,13 +109,14 @@
             device_id={"leaf": leaf_peers[0]}, device_id_type=MESH,
         ).wait_recv()
 
-    def joined(apply, base, into):
-        tiles = [None] * TILES
+    def joined(apply, turn, into):
+        tiles = [None, None]
 
         def put(tile, value):
             tiles[tile] = value if tiles[tile] is None else tiles[tile] + value
 
-        for i in range(EACH):
+        base = plane(turn) * X
+        for i in range(X):
             tile, offset = divmod(i * RANK, LANES)
             value = jnp.where(lane < RANK, into[apply, base + i].astype(F32), 0.0)
             if offset:
@@ -144,7 +126,14 @@
                 put(tile + 1, jnp.where(lane < offset, value, 0.0))
             else:
                 put(tile, value)
-        return jnp.concatenate(tiles, axis=1).astype(BF16)
+        return jnp.concatenate(tiles, axis=1).astype(BF16)[:, :PLANE]
+
+    def received(apply, turns, into, factor):
+        total = None
+        for turn in turns:
+            product = nn_dot(joined(apply, turn, into), factor[plane(turn)])
+            total = product if total is None else total + product
+        return total
 
     def rows_copy(src, dst, sems, r):
         return pltpu.make_async_remote_copy(
@@ -193,7 +182,7 @@
     pl.semaphore_wait(barrier, len(LEAF_STEPS) + len(ROW_STEPS))
     for n, q in enumerate(leaf_peers):
         a_out[0, n] = first_slots[perm[q]].astype(BF16)
-        leaf_send(0, n, a_out, a_in, a_send, a_recv.at[0], q)
+        leaf_send(0, n, a_out, a_in, a_send, a_recv.at[0, int(LEAF_STEPS[n][0] in FAR_TURNS)], q)
     a_in[0, leaf] = first_slots[perm[leaf]].astype(BF16)
 
     @pl.when(leaf >= 0)
@@ -217,8 +206,8 @@
                 col_t[g, pl.ds(first, count), :] = turned[start : start + count]
                 start += count
         for q in range(LEAVES):
-            c, i = divmod(q, EACH)
-            back_q[0, c, pl.ds(i * RANK, RANK), :] = col_t[perm[q]]
+            p, i = divmod(q, X)
+            back_q[0, p, pl.ds(i * RANK, RANK), :] = col_t[perm[q]]
         l_diag.wait()
         diag_points = jnp.broadcast_to(diag[...], (SIDES, PTS))
         diag_tree = [nn_dot(part, onehot[...]) for part in three_parts(diag_points)]
@@ -249,14 +238,14 @@
             gram_low[pl.ds(j * RANK, RANK), :] = (whole - high.astype(F32)).astype(BF16)
 
     def build_returner(kind):
-        for c in range(CHUNKS):
-            rows = pl.ds(c * GROUP, GROUP)
-            product = nt_dot(gram_high[...], weight[kind, rows]) + nt_dot(gram_low[...], weight[kind, rows])
-            returner[kind, :, c * GROUP : (c + 1) * GROUP] = product.astype(BF16)
-
-    def build_last(chunks):
-        for c in chunks:
-            back_q[1, c] = nt_dot(back_q[0, c], onehot[...]).astype(BF16)
+        for pair in range(Z // 2):
+            rows = jnp.concatenate([weight[kind, 2 * pair], weight[kind, 2 * pair + 1]], axis=0)
+            product = nt_dot(gram_high[...], rows) + nt_dot(gram_low[...], rows)
+            returner[kind, :, pair * GROUP : (pair + 1) * GROUP] = product.astype(BF16)
+
+    def build_last(planes):
+        for p in planes:
+            back_q[1, p] = nt_dot(back_q[0, p], onehot[...]).astype(BF16)
 
     earlier_head = None
     dots_total = None
@@ -276,9 +265,10 @@
                     rows_copy(dots_out, dots_in.at[row], dots_sems, r).start()
                 dots_in[row] = out
 
-        leaf_wait(apply, LEAVES - 1, a_in, a_send, a_recv.at[apply])
-        incoming = jnp.concatenate([joined(apply, c * EACH, a_in) for c in range(CHUNKS)], axis=1)
-        partial = nn_dot(incoming, weight[kind])
+        leaf_wait(apply, NEAR_COUNT, a_in, a_send, a_recv.at[apply, 0])
+        partial = received(apply, NEAR_TURNS, a_in, weight.at[kind])
+        leaf_wait(apply, FAR_COUNT, a_in, a_send, a_recv.at[apply, 1])
+        partial = partial + received(apply, FAR_TURNS, a_in, weight.at[kind])
         b_out[apply] = partial
         for r in row_peers:
             rows_copy(b_out.at[apply], b_in.at[apply, row], b_sems.at[apply], r).start()
@@ -308,40 +298,39 @@
                 + pltpu.roll(low.astype(F32), 80, 1)
             )
         put_slots(0, nn_dot(head, returner[kind]), extra)
-        send_peers(apply, 0, far_peers, c_out, c_in, c_send, lambda zz: c_recv.at[apply, 2])
-        send_peers(apply, EACH, near_peers, c_out, c_in, c_send, lambda zz: c_recv.at[apply, group_of(zz)])
+        send_peers(apply, FAR_TURNS + NEAR_TURNS, c_out, c_in, c_send, c_recv)
         c_in[apply, leaf] = slots[leaf].astype(BF16)
         @pl.when(leaf >= 0)
         def _():
             if apply == 0:
-                for c in range(CHUNKS):
-                    col_q[c] = back_q[0, c].T
+                for p in range(Z):
+                    col_q[p] = back_q[0, p].T
                 build_returner(1)
             if apply in (1, 2):
-                build_last((0, 1) if apply == 1 else (2, 3))
-
-        image = None
-        for group, (steps, count) in enumerate((((0,), EACH - 1), ((1, 3), 2 * EACH), ((2,), EACH))):
-            leaf_wait(apply, count, c_in, c_send, c_recv.at[apply, group])
-            for step in steps:
-                c = chunk(step)
-                product = nn_dot(joined(apply, c * EACH, c_in), back_q[1 if last else 0, c])
-                image = product if image is None else image + product
-                if last:
-                    for i in range(EACH):
-                        value = c_in[apply, c * EACH + i].astype(F32)
-                        dots_total = value if dots_total is None else dots_total + value
+                build_last(range(4) if apply == 1 else range(4, 8))
+
+        factor = back_q.at[int(last)]
+        leaf_wait(apply, NEAR_COUNT, c_in, c_send, c_recv.at[apply, 0])
+        image = received(apply, NEAR_TURNS, c_in, factor)
+        if last:
+            for q in [plane(turn) * X + i for turn in NEAR_TURNS for i in range(X)]:
+                value = c_in[apply, q].astype(F32)
+                dots_total = value if dots_total is None else dots_total + value
+        leaf_wait(apply, FAR_COUNT, c_in, c_send, c_recv.at[apply, 1])
+        image = image + received(apply, FAR_TURNS, c_in, factor)
+        if last:
+            for q in [plane(turn) * X + i for turn in FAR_TURNS for i in range(X)]:
+                dots_total = dots_total + c_in[apply, q].astype(F32)
         if not last:
             following = scale[kind] * field[apply] + image
             field[apply + 1] = following
             taken = following.astype(BF16)
-            c = chunk(2)
-            put_slots(c * EACH, nn_dot(taken, col_q[c]), zero)
-            send_peers(apply + 1, 0, far_peers, a_out, a_in, a_send, lambda zz: a_recv.at[apply + 1])
-            others = [(chunk(step), nn_dot(taken, col_q[chunk(step)])) for step in (1, 3, 0)]
-            for c, values in others:
-                put_slots(c * EACH, values, zero)
-            send_peers(apply + 1, EACH, near_peers, a_out, a_in, a_send, lambda zz: a_recv.at[apply + 1])
+            for turns in (FAR_TURNS, NEAR_TURNS):
+                for turn in turns:
+                    values = nn_dot(taken, col_q[plane(turn)])
+                    values = jnp.concatenate([values, jnp.zeros((SIDES, 2 * LANES - PLANE), F32)], axis=1)
+                    put_slots(plane(turn) * X, values, zero)
+                send_peers(apply + 1, turns, a_out, a_in, a_send, a_recv)
             a_in[apply + 1, leaf] = slots[leaf].astype(BF16)
 
     def dot_value(i):
@@ -370,7 +359,7 @@
         for out, send in ((a_out, a_send), (c_out, c_send)):
             pltpu.make_async_remote_copy(
                 src_ref=out.at[apply], dst_ref=out.at[apply],
-                send_sem=send.at[apply], recv_sem=a_recv.at[apply],
+                send_sem=send.at[apply], recv_sem=a_recv.at[apply, 0],
                 device_id={"leaf": leaf_peers[0]}, device_id_type=MESH,
             ).wait_send()
         for r in row_peers:
@@ -383,6 +372,7 @@
     hbm = pl.BlockSpec(memory_space=pl.ANY)
     vmem = pl.BlockSpec(memory_space=pltpu.VMEM)
     diagonal, tree_order = diagonal.reshape(1, PTS), tree_order.reshape(1, PTS)
+    mid_factor, pre_factor = mid_factor.reshape(Z, PLANE, GROUP), pre_factor.reshape(Z, PLANE, GROUP)
     right_side, diagonal, tree_order, mid_perm, col_factor, mid_factor, pre_factor, row_factor = (
         pltpu.with_memory_space_constraint(array, pltpu.HBM)
         for array in (right_side, diagonal, tree_order, mid_perm, col_factor, mid_factor, pre_factor, row_factor)
@@ -399,9 +389,9 @@
             pltpu.SMEM((LEAVES,), jnp.int32),
             pltpu.VMEM((PTS, LEAVES * RANK), BF16),
             pltpu.VMEM((LEAVES, RANK, PTS), BF16),
-            pltpu.VMEM((CHUNKS, PTS, GROUP), BF16),
-            pltpu.VMEM((2, CHUNKS, GROUP, PTS), BF16),
-            pltpu.VMEM((2, LEAVES * RANK, GROUP), BF16),
+            pltpu.VMEM((Z, PTS, PLANE), BF16),
+            pltpu.VMEM((2, Z, PLANE, PTS), BF16),
+            pltpu.VMEM((2, Z, PLANE, GROUP), BF16),
             pltpu.VMEM((2, GROUP, LEAVES * RANK), BF16),
             pltpu.VMEM((RANK, PTS), BF16),
             pltpu.VMEM((PTS, PTS), BF16),
@@ -427,10 +417,10 @@
             pltpu.SemaphoreType.DMA((2,)),
             pltpu.SemaphoreType.DMA((2,)),
             pltpu.SemaphoreType.DMA((APPLIES,)),
+            pltpu.SemaphoreType.DMA((APPLIES, 2)),
+            pltpu.SemaphoreType.DMA((APPLIES, 2)),
             pltpu.SemaphoreType.DMA((APPLIES,)),
             pltpu.SemaphoreType.DMA((APPLIES, 2)),
-            pltpu.SemaphoreType.DMA((APPLIES,)),
-            pltpu.SemaphoreType.DMA((APPLIES, 3)),
         ],
         compiler_params=pltpu.CompilerParams(
             collective_id=0, has_side_effects=True, vmem_limit_bytes=40000 * 1024

time: 78.8 us -> 77.9 us (0.989)
  Pallas kernels: 77.4 us -> 76.5 us
    pallas_call x1, Pallas kernels: 77.4 us -> 76.5 us  [per_device(): pl.pallas_call(kernel, out_shape=(jax.ShapeDtypeStruct((SIDES, PTS), F32)...]
where the time goes in v1:
time: 77.9 us; the launch traced here: 77.8 us
  Pallas kernels  76.5 us (98%)
    pallas_call x1, Pallas kernels, per_device(): pl.pallas_call(kernel, out_shape=(jax.ShapeDtypeStruct((SIDES, PTS), F32)...  76.5 us

profile of v1, /device:TPU:1, one launch (start us, length us, event | category | flops | bytes accessed | tf_op | source)
XLA Modules:
  0.0 77.8 jit_solution(15650918255072846012)
XLA Ops:
  0.6 76.5 %shard_map.95 = (f32[8,1024]{1,0:T(8,128)S(1)}, f32[8,1024]{1,0:T(8,128)S(1)}, f32[8,1024]{1,0:T(8,128)S(1)}, f32[8,1024]{1,0:T(8,128)S(1)}, f32[8,1024]{1,0:T(8,128)S(1)}) custom-call(f32[8,1024]{1,0:T(8,128)} %rs_hbm.1, f32[1,1024]{1,0:T(1,128)} %bitcast.6, s32[1,1024]{1,0:T(1,128)} %bitcast.7, s32[32]{0:T(128)} %perm_hbm.1, bf16[1024,1536]{1,0:T(8,128)(2,1)} %col_hbm.1, ...), custom_call_target="tpu_custom_call" | custom-call | tf_op jit(solution)/shard_map/pallas_call | solution.py:380
  77.1 0.6 multiply_subtract_fusion
